TPU v7x, 32 devices: a 4x4x1 block of a 4x4x8 slice. The times are simulated.
32 devices in a mesh: dp: 1 (over z), tp: 32 (over x, y, core).
Axes of the slice: x: 4, y: 4, z: 1, core: 2. Of those that a mesh axis runs over, the one named last changes fastest.
The devices are a block of a 4x4x8 slice.
Arguments:
- x: bfloat16 [4096, 8192], P(('dp', 'tp'))
- w_gate: bfloat16 [8192, 49152], P(None, 'tp')
- w_up: bfloat16 [8192, 49152], P(None, 'tp')
- w_down: bfloat16 [49152, 8192], P('tp')
Outputs:
- output: bfloat16 [4096, 8192], P(('dp', 'tp'))
All inputs are finite; a program needn't handle non-finite values.
Results may differ from a plain program's by a relative error of at most 0.016.
Values are sent between devices in bfloat16 or wider.
A program may use at most 768 MiB of HBM per device.

v0:
```python
import jax
import jax.numpy as jnp
from jax import lax
from jax.sharding import PartitionSpec as P


def solution(mesh):
    def step(x, w_gate, w_up, w_down):
        rows = lax.all_gather(x, "tp", axis=0, tiled=True)
        gate = jnp.dot(rows, w_gate, preferred_element_type=jnp.float32)
        up = jnp.dot(rows, w_up, preferred_element_type=jnp.float32)
        hidden = (jax.nn.silu(gate) * up).astype(jnp.bfloat16)
        term = jnp.dot(hidden, w_down, preferred_element_type=jnp.float32).astype(jnp.bfloat16)
        return lax.psum_scatter(term, "tp", scatter_dimension=0, tiled=True)

    return jax.shard_map(
        step,
        mesh=mesh,
        in_specs=(P(("dp", "tp"), None), P(None, "tp"), P(None, "tp"), P("tp", None)),
        out_specs=P(("dp", "tp"), None),
        check_vma=False,
    )
```

profile of v0, /device:TPU:97, one launch (start us, length us, event | category | flops | bytes accessed | tf_op | source)
XLA Modules:
  0.0 850.1 jit_solution(15143518056748765348)
XLA Ops:
  6.5 0.0 all-gather.2.cloned.1.call-start
  6.6 0.7 all-gather.2.cloned.1.call-update
  7.3 0.1 reduce-scatter.4.cloned.1.call-start
  7.4 202.2 %all-gather.2.cloned.1.call-done = bf16[4096,8192]{1,0:T(8,128)(2,1)} async-done(((bf16[128,8192]{1,0:T(8,128)(2,1)}), bf16[4096,8192]{1,0:T(8,128)(2,1)}) %all-gather.2.cloned.1.call-update) | async-done | bytes 67108880 | tf_op jit(solution)/shard_map/all_gather | solution.py:9
  209.6 117.1 %fusion = f32[4096,1536]{1,0:T(8,128)} fusion(bf16[4096,8192]{1,0:T(8,128)(2,1)} %all-gather.2.cloned.1.call-done, bf16[8192,1536]{1,0:T(8,128)(2,1)} %param.5), kind=kOutput, calls=%fused_computation.2 | convolution fusion | flops 103079215104 | bytes 117440512 | tf_op jit(solution)/shard_map/dot_general | solution.py:10
  326.7 118.5 %multiply_convert_fusion = bf16[4096,1536]{1,0:T(8,128)(2,1)} fusion(f32[4096,1536]{1,0:T(8,128)} %fusion, bf16[4096,8192]{1,0:T(8,128)(2,1)} %all-gather.2.cloned.1.call-done, bf16[8192,1536]{1,0:T(8,128)(2,1)} %param.6), kind=kOutput, calls=%fused_computation.1 | convolution fusion | flops 103116963840 | bytes 130023424 | tf_op jit(solution)/shard_map/dot_general | solution.py:11
  445.2 115.0 %convolution_convert_fusion = bf16[4096,8192]{1,0:T(8,128)(2,1)} fusion(bf16[4096,1536]{1,0:T(8,128)(2,1)} %multiply_convert_fusion, bf16[1536,8192]{1,0:T(8,128)(2,1)} %param.7), kind=kOutput, calls=%fused_computation | convolution fusion | flops 103112769536 | bytes 104857600 | tf_op jit(solution)/shard_map/dot_general | solution.py:13
  560.2 0.1 reduce-scatter.4.cloned.1.call-update
  560.3 283.0 %reduce-scatter.4.cloned.1.call-done = bf16[128,8192]{1,0:T(8,128)(2,1)} async-done(((bf16[4096,8192]{1,0:T(8,128)(2,1)}), bf16[128,8192]{1,0:T(8,128)(2,1)}) %reduce-scatter.4.cloned.1.call-update) | async-done | bytes 2097168
Async XLA Ops:
  6.5 203.0 %all-gather.2.cloned.1.call-start = ((), (), s32[]{:S(2)}) async-start(), calls=%async_computation.1 | async-start | bytes 69206016 | tf_op jit(solution)/shard_map/all_gather | solution.py:9
  7.3 836.0 %reduce-scatter.4.cloned.1.call-start = ((), (), s32[]{:S(2)}) async-start(), calls=%async_computation.2 | async-start | bytes 69206016
Sparse Core Ops, SparseCore 0:
  9.4 200.1 all-gather.1
  560.4 282.8 reduce-scatter.3
where the time goes:
time: 850 us
  waiting for transfers between devices  486 us (57%)
  matrix products  351 us (41%)
  between operations  13.4 us (2%)
    unnamed x3, waiting for transfers between devices  284 us
    all_gather x1, waiting for transfers between devices, step(): rows = lax.all_gather(x, 'tp', axis=0, tiled=True)  202 us
    dot_general x1, matrix products, step(): up = jnp.dot(rows, w_up, preferred_element_type=jnp.float32)  118 us
    dot_general x1, matrix products, step(): gate = jnp.dot(rows, w_gate, preferred_element_type=jnp.float32)  117 us
    dot_general x1, matrix products, step(): jnp.dot(hidden, w_down, preferred_element_type=jnp.float32)  115 us
  transfers between devices with their start and end apart: 2, of which 2 were waited for; matrix products, arithmetic and copies ran while one was open for 0% of the time, Pallas kernels for 0%

commit v1 on v0

v1 whole, which is shorter than its diff:
```python
import functools
import math

import jax
import jax.numpy as jnp
from jax import lax
from jax.experimental import pallas as pl
from jax.experimental.pallas import tpu as pltpu
from jax.sharding import PartitionSpec as P

F32, BF16 = jnp.float32, jnp.bfloat16


def kernel(side, tn, dt, x, wg, wu, wd, y, xs, wp, rs, wbuf, h0, hk, hs, out, inb, ab, bb, wsem, xsem, isem, ysem,
           ag_s, ag_r, pu_s, pu_r, wp_s, wp_r, hx_s, hx_r, rs_s, rs_r, a_s, a_r, b_s, b_r, hfree):
    rows, d = x.shape
    hid = wg.shape[1]
    hr = rows // 2
    half_rows = side * hr
    nt, nd = hid // tn, d // dt
    sub = dt // tn
    part_cols = hid // 2
    wp_rows = hid // nt

    t = lax.axis_index("tp")
    c = lax.rem(t, 2)
    cx, cy = t // (2 * side), lax.rem(t // 2, side)
    f, s = cx * (1 - c) + cy * c, cy * (1 - c) + cx * c

    def at(df, ds):
        ff, ss = lax.rem(f + df + side, side), lax.rem(s + ds + side, side)
        return ((ff * (1 - c) + ss * c) * side + ss * (1 - c) + ff * c) * 2 + c

    fp, fm, sp, sm, sib = at(1, 0), at(-1, 0), at(0, 1), at(0, -1), t + 1 - 2 * c

    def remote(src, dst, send, recv, dev):
        return pltpu.make_async_remote_copy(src_ref=src, dst_ref=dst, send_sem=send, recv_sem=recv, device_id={"tp": dev})

    def when(cond):
        return pl.when(cond)

    def row0(j, hf):
        return hf * half_rows + j * hr

    def piece(k, j, hf, other=0):
        return xs.at[other, k, pl.ds(row0(j, hf), hr)]

    def source(k, j, hf):
        if isinstance(k, int) and isinstance(j, int) and k == 0 and j == 0:
            return x.at[pl.ds(hf * hr, hr)]
        return piece(k, j, hf)

    def move(src, k, j, hf, dev):
        i = j * 2 + hf
        return remote(src, piece(k, j, hf), ag_s.at[k, i], ag_r.at[k, i], dev)

    def hand(k, j, hf):
        i = j * 2 + hf
        return remote(source(k, j, hf), piece(k, j, hf, 1), pu_s.at[k, i], pu_r.at[k, i], sib)

    def arrive(k, j, hf):
        move(piece(k, j, hf), k, j, hf, sib).wait_recv()
        hand(k, j, hf).start()

    def push(k, j):
        for hf in range(2):
            arrive(k, j, hf)

    def forward(k, j):
        for hf, dev in ((0, sp), (1, sm)):
            move(source(k, j, hf), k + 1, j, hf, dev).start()

    def far():
        move(piece(0, 1, 0), 0, 3, 0, fp).start()
        move(piece(0, 2, 1), 0, 3, 1, fm).start()

    def load(xb, slot, i, k, j, n):
        hf = i % 2
        seg = n * hr
        if i < 2:
            src = x.at[pl.ds(hf * hr, hr)] if n == 1 and isinstance(j, int) and j == 0 else xs.at[0, k, pl.ds(row0(j, hf), seg)]
        else:
            src = xs.at[1, k, pl.ds(row0(j, hf), seg)]
        return pltpu.make_async_copy(src, xb.at[slot, pl.ds(i * seg, seg)], xsem.at[slot, i])

    def load_start(xb, slot, i, k, j, n):
        if i >= 2:
            for q in range(n):
                hand(k, j + q, i % 2).wait_recv()
        load(xb, slot, i, k, j, n).start()

    def u_copies(n, slot):
        cols = pl.ds(pl.multiple_of(n * tn, tn), tn)
        return [pltpu.make_async_copy(w.at[:, cols], wbuf.at[slot, i], wsem.at[slot, i]) for i, w in enumerate((wg, wu))]

    def d_rows(q):
        return q // 2, (q % 2) * 2 * hid

    def d_copies(n, slot):
        r = []
        for q in range(sub):
            p, o = d_rows(q)
            cols = pl.ds(pl.multiple_of(n * dt + q * tn, tn), tn)
            for i, w in enumerate((wd, wp)):
                r.append(pltpu.make_async_copy(w.at[:, cols], wbuf.at[slot, p, pl.ds(o + i * hid, hid)], wsem.at[slot, 2 * q + i]))
        return r

    def start(copies):
        for cp in copies:
            cp.start()

    def wait(copies):
        for cp in copies:
            cp.wait()

    def h_copy(hdst, slot, j, n, part, hf, idx):
        seg, i = n * hr, part * 2 + hf
        cols = part * part_cols
        return remote(hs.at[slot, pl.ds(hf * seg, seg), pl.ds(cols, part_cols)],
                      hdst.at[pl.ds(row0(j, hf), seg), pl.ds(hid + cols, part_cols)],
                      hx_s.at[slot, i], hx_r.at[idx, i], sib)

    def h_push(hdst, slot, j, n, part, idx):
        for hf in range(2):
            h_copy(hdst, slot, j, n, part, hf, idx).start()

    def h_sent(slot, n):
        for part in range(2):
            for hf in range(2):
                h_copy(h0, slot, 0, n, part, hf, 0).wait_send()

    def h_here(idx, n):
        for part in range(2):
            for hf in range(2):
                h_copy(h0, 0, 0, n, part, hf, idx).wait_recv()

    def u_phase(xb, slot, hdst, j, n, idx, hook, nxt):
        seg = n * hr
        m = 4 * seg

        def body(i, carry):
            ws = lax.rem(i, 2)
            hook(i)

            @when(i == nt // 2)
            def _():
                h_push(hdst, slot, j, n, 0, idx)

            @when(i < nt - 1)
            def _():
                start(u_copies(i + 1, 1 - ws))

            @when(i == nt - 1)
            def _():
                nxt()

            @when(i == 0)
            def _():
                for q in range(4):
                    load(xb, slot, q, 0, 1, n).wait()

            wait(u_copies(i, ws))
            lhs = xb.at[slot, pl.ds(0, m)]
            gate = jnp.dot(lhs[...], wbuf[ws, 0], preferred_element_type=F32)
            up = jnp.dot(lhs[...], wbuf[ws, 1], preferred_element_type=F32)
            hidden = (jax.nn.silu(gate) * up).astype(BF16)
            cols = pl.ds(pl.multiple_of(i * tn, tn), tn)
            for hf in range(2):
                hdst[pl.ds(row0(j, hf), seg), cols] = hidden[hf * seg : (hf + 1) * seg]
            hs[slot, pl.ds(0, 2 * seg), cols] = hidden[2 * seg :]
            return carry

        lax.fori_loop(0, nt, body, 0)
        h_push(hdst, slot, j, n, 1, idx)

    def sum_copy(hop, n, hf):
        part = pl.ds(hf * half_rows, half_rows)
        return remote(out.at[n, part], rs.at[hop, n, part], rs_s.at[n, hf], rs_r.at[hop, 2 * n + hf], (sp, sm)[hf])

    def in_copy(hop, n):
        b = lax.rem(n, 2)
        return pltpu.make_async_copy(rs.at[hop, n], inb.at[b], isem.at[b])

    def in_start(hop, n):
        for hf in range(2):
            sum_copy(hop, n, hf).wait_recv()
        in_copy(hop, n).start()

    def products(h, n, q):
        p, o = d_rows(q)
        ws = lax.rem(n, 2)
        cols = slice(q * tn, (q + 1) * tn)
        term = jnp.dot(h[...], wbuf[ws, p, pl.ds(o, 2 * hid)], preferred_element_type=F32)
        return term + inb[lax.rem(n, 2), :, cols].astype(F32), cols

    def a_copy(n, hf):
        return remote(out.at[n, pl.ds(hf * hr, hr)], ab.at[n, hf], a_s.at[n, hf], a_r.at[n, hf], (fp, fm)[hf])

    def b_copy(n, i):
        return remote(out.at[n, pl.ds((1 + i) * rows, rows)], bb.at[n, i], b_s.at[n, i], b_r.at[n, i], (fp, fm)[i])

    def y_copy(n):
        cols = pl.ds(pl.multiple_of(n * dt, dt), dt)
        return pltpu.make_async_copy(out.at[n, pl.ds(3 * rows, rows)], y.at[:, cols], ysem.at[n])

    start(u_copies(0, 0))
    barrier = pltpu.get_barrier_semaphore()
    for dev in (fp, fm, sp, sm, sib):
        pl.semaphore_signal(barrier, 1, device_id={"tp": dev})
    pl.semaphore_wait(barrier, 5)

    for hf in range(2):
        hand(0, 0, hf).start()
    for hf in range(2):
        move(source(0, 0, hf), 0, 1, hf, fp).start()
        move(source(0, 0, hf), 0, 2, hf, fm).start()
    inb[...] = jnp.zeros_like(inb)

    def rounds(xb):
        for i in range(4):
            load_start(xb, 0, i, 0, 0, 1)

        def hook(i):
            @when(i == nt - 2)
            def _():
                arrive(0, 1, 0)
                arrive(0, 2, 0)

        u_phase(xb, 0, h0, 0, 1, 0, hook, lambda: start(u_copies(0, 0)))

        arrive(0, 1, 1)
        arrive(0, 2, 1)
        for j in range(3):
            forward(0, j)
        for i in range(4):
            load_start(xb, 1, i, 0, 1, 2)

        def hook(i):
            @when(i == 3)
            def _():
                push(1, 0)

            @when(i == 4)
            def _():
                far()

            @when(i == 5)
            def _():
                push(1, 1)

        u_phase(xb, 1, h0, 1, 2, 1, hook, lambda: start(u_copies(0, 0)))
        for i in range(4):
            load_start(xb, 0, i, 1, 0, 2)

        def one_round(k, carry):
            def chunk(b, carry):
                @when((k == 1) & (b == 0))
                def _():
                    h_sent(0, 1)

                @when((k > 1) | (b == 1))
                def _():
                    h_sent(b, 2)

                @when((k == 1) & (b == 1))
                def _():
                    push(1, 3)
                    for i in range(4):
                        load_start(xb, 1, i, 1, 2, 2)

                def hook(i):
                    @when((k == 1) & (b == 0))
                    def _():
                        piece_rows = pl.ds(i * wp_rows, wp_rows)
                        remote(wd.at[piece_rows], wp.at[piece_rows], wp_s.at[i], wp_r.at[i], sib).start()

                        @when(i == 3)
                        def _():
                            push(0, 3)
                            forward(0, 3)

                        @when(i == 4)
                        def _():
                            push(1, 2)
                            forward(1, 0)

                        @when(i == 5)
                        def _():
                            forward(1, 1)

                    @when((k == 1) & (b == 1))
                    def _():
                        @when(i == 0)
                        def _():
                            forward(1, 2)

                        @when(i == 1)
                        def _():
                            forward(1, 3)

                        @when(i == 3)
                        def _():
                            push(2, 0)

                        @when(i == 5)
                        def _():
                            push(2, 1)
                            forward(2, 0)

                    @when((k == 2) & (b == 1))
                    def _():
                        @when(i == 1)
                        def _():
                            push(3, 0)

                        @when(i == 3)
                        def _():
                            push(3, 1)

                        @when(i == 5)
                        def _():
                            push(3, 2)

                    @when((k > 1) & (b == 0))
                    def _():
                        @when(i == nt // 2)
                        def _():
                            pl.semaphore_wait(hfree, 1)

                        for q in range(4):
                            @when(i == 2 + q)
                            def _():
                                load_start(xb, 1, q, k, 2, 2)

                    @when((k > 1) & (b == 1) & (i == nt - 2))
                    def _():
                        in_start(k - 2, 0)

                def nxt():
                    @when(b == 0)
                    def _():
                        start(u_copies(0, 0))

                    @when(b == 1)
                    def _():
                        @when(k == 1)
                        def _():
                            for i in range(nt):
                                piece_rows = pl.ds(i * wp_rows, wp_rows)
                                remote(wd.at[piece_rows], wp.at[piece_rows], wp_s.at[i], wp_r.at[i], sib).wait_recv()

                        start(d_copies(0, 0))

                u_phase(xb, b, hk, 2 * b, 2, 2 + b, hook, nxt)
                return carry

            lax.fori_loop(0, 2, chunk, 0)
            h_here(2, 2)
            h_here(3, 2)

            def down(n, carry):
                ws = lax.rem(n, 2)

                @when(n < nd - 1)
                def _():
                    start(d_copies(n + 1, 1 - ws))

                @when(n == nd - 1)
                def _():
                    start(u_copies(0, 0))

                @when(k > 1)
                def _():
                    in_copy(k - 2, n).wait()

                    @when(n < nd - 1)
                    def _():
                        in_start(k - 2, n + 1)

                    for hf in range(2):
                        sum_copy(0, n, hf).wait_send()

                @when(k == 1)
                def _():
                    @when(n == 1)
                    def _():
                        push(2, 2)
                        forward(2, 1)

                    @when(n == 3)
                    def _():
                        forward(2, 2)

                    @when(n == 5)
                    def _():
                        push(2, 3)
                        forward(2, 3)

                @when((k == 2) & (n == 1))
                def _():
                    push(3, 3)

                @when(k < 3)
                def _():
                    for q in range(4):
                        @when(n == 2 + q)
                        def _():
                            load_start(xb, 0, q, k + 1, 0, 2)

                @when(k == 3)
                def _():
                    for q in range(4):
                        @when(n == 2 + q)
                        def _():
                            load_start(xb, 0, q, 0, 3, 1)

                wait(d_copies(n, ws))
                for q in range(sub):
                    total, cols = products(hk, n, q)
                    out[n, :, cols] = total.astype(BF16)
                for hf in range(2):
                    sum_copy(k - 1, n, hf).start()
                return carry

            lax.fori_loop(0, nd, down, 0)

            @when(k < 3)
            def _():
                pl.semaphore_signal(hfree, 1, device_id={"tp": sib})

            return carry

        lax.fori_loop(1, side, one_round, 0)

        def hook(i):
            @when(i == nt - 2)
            def _():
                in_start(2, 0)

        h_sent(0, 2)
        u_phase(xb, 0, h0, 3, 1, 4, hook, lambda: start(d_copies(0, 0)))

    pl.run_scoped(rounds, pltpu.VMEM((2, 8 * hr, d), BF16))

    def last(t0, t1, t2):
        h_here(0, 1)
        h_here(1, 2)
        h_here(4, 1)

        def add_far(n):
            for hf in range(2):
                a_copy(n, hf).wait_recv()
            out[n, pl.ds(rows, hr)] = (t2[n, :hr] + ab[n, 0].astype(F32)).astype(BF16)
            out[n, pl.ds(rows + hr, hr)] = t2[n, hr:].astype(BF16)
            out[n, pl.ds(2 * rows, hr)] = t1[n, :hr].astype(BF16)
            out[n, pl.ds(2 * rows + hr, hr)] = (t1[n, hr:] + ab[n, 1].astype(F32)).astype(BF16)
            for i in range(2):
                b_copy(n, i).start()

        def add_near(n):
            for i in range(2):
                b_copy(n, i).wait_recv()
            out[n, pl.ds(3 * rows, rows)] = (t0[n] + bb[n, 0].astype(F32) + bb[n, 1].astype(F32)).astype(BF16)
            y_copy(n).start()

        def down(n, carry):
            ws = lax.rem(n, 2)

            @when(n < nd - 1)
            def _():
                start(d_copies(n + 1, 1 - ws))

            in_copy(2, n).wait()

            @when(n < nd - 1)
            def _():
                in_start(2, n + 1)

            for hf in range(2):
                sum_copy(0, n, hf).wait_send()

            @when(n >= 2)
            def _():
                add_far(n - 2)

            @when(n >= 5)
            def _():
                add_near(n - 5)

            wait(d_copies(n, ws))
            for q in range(sub):
                total, cols = products(h0, n, q)
                for hf in range(2):
                    o = hf * half_rows
                    dst = pl.ds(hf * hr, hr)
                    t0[n, dst, cols] = total[o : o + hr]
                    t1[n, dst, cols] = total[o + hr : o + 2 * hr]
                    t2[n, dst, cols] = total[o + 2 * hr : o + 3 * hr]
                    out[n, dst, cols] = total[o + 3 * hr : o + 4 * hr].astype(BF16)
            for hf in range(2):
                a_copy(n, hf).start()
            return carry

        lax.fori_loop(0, nd, down, 0)

        def drain(n, carry):
            @when(n < nd)
            def _():
                add_far(n)

            add_near(n - 3)
            return carry

        lax.fori_loop(nd - 2, nd + 3, drain, 0)

    shape = pltpu.VMEM((nd, rows, dt), F32)
    pl.run_scoped(last, shape, shape, shape)

    for n in range(nd):
        y_copy(n).wait()
        for i in range(2):
            a_copy(n, i).wait_send()
            b_copy(n, i).wait_send()
    h_sent(0, 1)
    h_sent(1, 2)
    for i in range(nt):
        piece_rows = pl.ds(i * wp_rows, wp_rows)
        remote(wd.at[piece_rows], wp.at[piece_rows], wp_s.at[i], wp_r.at[i], sib).wait_send()
    for k in range(side):
        for j in range(side):
            for hf in range(2):
                hand(k, j, hf).wait_send()
                if k or j:
                    move(piece(k, j, hf), k, j, hf, sib).wait_send()


def build(mesh, tn, dt):
    side = math.isqrt(mesh.shape["tp"] // 2)

    def step(x, w_gate, w_up, w_down):
        rows, d = x.shape
        hid = w_gate.shape[1]
        hr = rows // 2
        nt, nd = hid // tn, d // dt
        dma = pltpu.SemaphoreType.DMA
        hbm = pl.BlockSpec(memory_space=pltpu.HBM)
        m = side * rows
        result = pl.pallas_call(
            functools.partial(kernel, side, tn, dt),
            out_shape=(
                jax.ShapeDtypeStruct((rows, d), BF16),
                jax.ShapeDtypeStruct((2, side, m, d), BF16),
                jax.ShapeDtypeStruct((hid, d), BF16),
                jax.ShapeDtypeStruct((side - 1, nd, m, dt), BF16),
            ),
            in_specs=[hbm] * 4,
            out_specs=[hbm] * 4,
            scratch_shapes=[
                pltpu.VMEM((2, 2, d, tn), BF16),
                pltpu.VMEM((m, 2 * hid), BF16),
                pltpu.VMEM((m, 2 * hid), BF16),
                pltpu.VMEM((2, 4 * hr, hid), BF16),
                pltpu.VMEM((nd, m, dt), BF16),
                pltpu.VMEM((2, m, dt), BF16),
                pltpu.VMEM((nd, 2, hr, dt), BF16),
                pltpu.VMEM((nd, 2, rows, dt), BF16),
                dma((2, 2 * dt // tn)),
                dma((2, 4)),
                dma((2,)),
                dma((nd,)),
                dma((side, 2 * side)),
                dma((side, 2 * side)),
                dma((side, 2 * side)),
                dma((side, 2 * side)),
                dma((nt,)),
                dma((nt,)),
                dma((2, 4)),
                dma((5, 4)),
                dma((nd, 2)),
                dma((side - 1, 2 * nd)),
                dma((nd, 2)),
                dma((nd, 2)),
                dma((nd, 2)),
                dma((nd, 2)),
                pltpu.SemaphoreType.REGULAR,
            ],
            compiler_params=pltpu.CompilerParams(collective_id=0, has_side_effects=True, vmem_limit_bytes=67043328),
            cost_estimate=pl.CostEstimate(flops=6 * side * side * 2 * rows * d * hid, bytes_accessed=9 * d * hid * 4, transcendentals=0),
            name="mlp",
        )(x, w_gate, w_up, w_down)
        return result[0]

    return jax.shard_map(
        step,
        mesh=mesh,
        in_specs=(P(("dp", "tp"), None), P(None, "tp"), P(None, "tp"), P("tp", None)),
        out_specs=P(("dp", "tp"), None),
        check_vma=False,
    )


def solution(mesh):
    return build(mesh, 256, 1024)
```

time: 850 us -> 412 us (0.48)
  waiting for transfers between devices: 486 us -> 0 us
  Pallas kernels: 0 us -> 408 us
  matrix products: 351 us -> 0 us
  between operations: 13.4 us -> 0.01 us
    pallas_call x0 -> x1, Pallas kernels: none -> 408 us  [step(): pl.pallas_call(functools.partial(kernel, side, tn, dt), out_shape=(jax.Sh...]
    dot_general x3 -> x0, matrix products: 351 us -> none  [the longest x1 118 us: step(): up = jnp.dot(rows, w_up, preferred_element_type=jnp.float32)]
    unnamed x3 -> x0, waiting for transfers between devices: 284 us -> none
    all_gather x1 -> x0, waiting for transfers between devices: 202 us -> none  [step(): rows = lax.all_gather(x, 'tp', axis=0, tiled=True)]
  transfers between devices with their start and end apart: 2 -> 0, of which waited for: 2 -> 0; matrix products, arithmetic and copies ran while one was open for 0% -> 0% of each run, Pallas kernels for 0% -> 0%
where the time goes in v1:
time: 412 us; the launch traced here: 411 us
  Pallas kernels  408 us (99%)
    pallas_call x1, Pallas kernels, step(): pl.pallas_call(functools.partial(kernel, side, tn, dt), out_shape=(jax.Sh...  408 us

profile of v1, /device:TPU:97, one launch (start us, length us, event | category | flops | bytes accessed | tf_op | source)
XLA Modules:
  0.0 411.1 jit_solution(6210168273721172658)
XLA Ops:
  0.0 408.0 %mlp.1 = (bf16[128,8192]{1,0:T(8,128)(2,1)}, bf16[2,4,512,8192]{3,2,1,0:T(8,128)(2,1)}, bf16[1536,8192]{1,0:T(8,128)(2,1)}, bf16[3,8,512,1024]{3,2,1,0:T(8,128)(2,1)}) custom-call(bf16[128,8192]{1,0:T(8,128)(2,1)} %x.1, bf16[8192,1536]{1,0:T(8,128)(2,1)} %wg.1, bf16[8192,1536]{1,0:T(8,128)(2,1)} %wu.1, bf16[1536,8192]{1,0:T(8,128)(2,1)} %wd.1), custom_call_target="tpu_custom_call" | custom-call | flops 309237645312 | bytes 452984832 | tf_op jit(solution)/shard_map/mlp/pallas_call | solution.py:548
  408.0 3.1 copy.6

commit v2 on v1

v2 whole, which is shorter than its diff:
```python
import functools
import math

import jax
import jax.numpy as jnp
from jax import lax
from jax.experimental import pallas as pl
from jax.experimental.pallas import tpu as pltpu
from jax.sharding import PartitionSpec as P

F32, BF16 = jnp.float32, jnp.bfloat16


def kernel(side, tn, dt, x, wg, wu, wd, y, xs, wp, rs, wbuf, h0, hk, out, inb, wsem, xsem, isem, ysem,
           ag_s, ag_r, pu_s, pu_r, wp_s, wp_r, hx_s, hx_r, hy_s, hy_r, rs_s, rs_r, a_s, a_r, b_s, b_r, hfree, nfree):
    rows, d = x.shape
    hid = wg.shape[1]
    hr = rows // 2
    half_rows = side * hr
    m = 2 * half_rows
    seg = 2 * hr
    nt, nd = hid // tn, d // dt
    sub = dt // tn
    cuts = (0, nt // 2, nt - 1, nt)
    parts = len(cuts) - 1
    pieces = wp_s.shape[0]

    t = lax.axis_index("tp")
    c = lax.rem(t, 2)
    cx, cy = t // (2 * side), lax.rem(t // 2, side)
    f, s = cx * (1 - c) + cy * c, cy * (1 - c) + cx * c

    def at(df, ds):
        ff, ss = lax.rem(f + df + side, side), lax.rem(s + ds + side, side)
        return ((ff * (1 - c) + ss * c) * side + ss * (1 - c) + ff * c) * 2 + c

    fp, fm, sp, sm, sib = at(1, 0), at(-1, 0), at(0, 1), at(0, -1), t + 1 - 2 * c

    def remote(src, dst, send, recv, dev):
        return pltpu.make_async_remote_copy(src_ref=src, dst_ref=dst, send_sem=send, recv_sem=recv, device_id={"tp": dev})

    def when(cond):
        return pl.when(cond)

    def row0(j, hf):
        return hf * half_rows + j * hr

    def piece(k, j, hf, other=0):
        return xs.at[other, k, pl.ds(row0(j, hf), hr)]

    def source(k, j, hf):
        if isinstance(k, int) and isinstance(j, int) and k == 0 and j == 0:
            return x.at[pl.ds(hf * hr, hr)]
        return piece(k, j, hf)

    def move(src, k, j, hf, dev):
        i = j * 2 + hf
        return remote(src, piece(k, j, hf), ag_s.at[k, i], ag_r.at[k, i], dev)

    def hand(k, j, hf):
        i = j * 2 + hf
        return remote(source(k, j, hf), piece(k, j, hf, 1), pu_s.at[k, i], pu_r.at[k, i], sib)

    def arrive(k, j, hf):
        move(piece(k, j, hf), k, j, hf, sib).wait_recv()
        hand(k, j, hf).start()

    def push(k, j):
        for hf in range(2):
            arrive(k, j, hf)

    def forward(k, j):
        for hf, dev in ((0, sp), (1, sm)):
            move(source(k, j, hf), k + 1, j, hf, dev).start()

    def far(k, hf):
        move(piece(k, 1 + hf, hf), k, 3, hf, (fp, fm)[hf]).start()

    def load(xb, slot, i, src, size):
        return pltpu.make_async_copy(src, xb.at[slot, pl.ds(i * size, size)], xsem.at[slot, i])

    def load_small(xb, slot, i, k, j, hf):
        if i < 2:
            src = source(k, j, hf)
        else:
            hand(k, j, hf).wait_recv()
            src = piece(k, j, hf, 1)
        load(xb, slot, i, src, hr).start()

    def load_mid(xb, slot, i):
        other, hf = i // 2, i % 2
        if other:
            for j in (1, 2):
                hand(0, j, hf).wait_recv()
        load(xb, slot, i, xs.at[other, 0, pl.ds(row0(1, hf), seg)], seg).start()

    def load_pair(xb, slot, i, other, k, pair, hf):
        for q in range(2):
            @when(other == 1)
            def _():
                hand(k, 2 * pair + q, hf).wait_recv()
        load(xb, slot, i, xs.at[other, k, pl.ds(hf * half_rows + pair * seg, seg)], seg).start()

    def loaded(xb, slot, size):
        for i in range(4):
            load(xb, slot, i, xs.at[0, 0, pl.ds(0, size)], size).wait()

    def u_part(n, z, slot):
        cols, depth = pl.ds(pl.multiple_of(n * tn, tn), tn), pl.ds(z * (d // 2), d // 2)
        return [pltpu.make_async_copy(w.at[depth, cols], wbuf.at[slot, i, depth], wsem.at[slot, 2 * z + i])
                for i, w in enumerate((wg, wu))]

    def u_copies(n, slot):
        return u_part(n, 0, slot) + u_part(n, 1, slot)

    def d_rows(q):
        return q // 2, (q % 2) * 2 * hid

    def d_copies(n, slot):
        r = []
        for q in range(sub):
            p, o = d_rows(q)
            cols = pl.ds(pl.multiple_of(n * dt + q * tn, tn), tn)
            for i, w in enumerate((wd, wp)):
                r.append(pltpu.make_async_copy(w.at[:, cols], wbuf.at[slot, p, pl.ds(o + i * hid, hid)], wsem.at[slot, 2 * q + i]))
        return r

    def start(copies):
        for cp in copies:
            cp.start()

    def wait(copies):
        for cp in copies:
            cp.wait()

    def cut(part):
        return cuts[part] * tn, (cuts[part + 1] - cuts[part]) * tn

    def h_copy(hdst, idx, part, q, src, dst, size):
        i = part * 2 + q
        lo, width = cut(part)
        return remote(hk.at[pl.ds(m + src, size), pl.ds(lo, width)], hdst.at[pl.ds(dst, size), pl.ds(hid + lo, width)],
                      hx_s.at[idx, i], hx_r.at[idx, i], sib)

    def h_push(hdst, idx, part, src, dst, size):
        for q in range(2):
            h_copy(hdst, idx, part, q, src[q], dst[q], size).start()

    def h_sent(idx, size):
        for part in range(parts):
            for q in range(2):
                h_copy(h0, idx, part, q, 0, 0, size).wait_send()

    def h_here(idx, size):
        for part in range(parts):
            for q in range(2):
                h_copy(h0, idx, part, q, 0, 0, size).wait_recv()

    def hy_copy(part):
        lo, size = cut(part)
        return remote(hk.at[pl.ds(m, m), pl.ds(lo, size)], hk.at[pl.ds(0, m), pl.ds(hid + lo, size)],
                      hy_s.at[part], hy_r.at[part], sib)

    def w_piece(i):
        r = pl.ds(i * (hid // pieces), hid // pieces)
        return remote(wd.at[r], wp.at[r], wp_s.at[i], wp_r.at[i], sib)

    def hidden(lhs, ws):
        gate = jnp.dot(lhs[...], wbuf[ws, 0], preferred_element_type=F32)
        up = jnp.dot(lhs[...], wbuf[ws, 1], preferred_element_type=F32)
        return (jax.nn.silu(gate) * up).astype(BF16)

    def u_cols(i):
        return pl.ds(pl.multiple_of(i * tn, tn), tn)

    def u_small(xb, slot, keep, where, idx, hook, ahead, nxt):
        half = d // 2

        def body(i, carry):
            ws = lax.rem(i, 2)
            hook(i)

            for part in range(parts - 1):
                @when(i == cuts[part + 1])
                def _():
                    h_push(h0, idx, part, keep, where, hr)

            if not ahead:
                @when(i == 0)
                def _():
                    start(u_part(1, 0, 1))

            if nxt:
                start(u_part(lax.rem(i + 1, nt), 1, 1 - ws))
            else:
                @when(i < nt - 1)
                def _():
                    start(u_part(i + 1, 1, 1 - ws))

                @when(i == nt - 1)
                def _():
                    start(d_copies(0, 0))

            @when(i == 0)
            def _():
                loaded(xb, slot, hr)

            rows4 = pl.ds(0, 4 * hr)

            def products_of(z):
                wait(u_part(i, z, ws))
                lhs, depth = xb[slot, rows4, pl.ds(z * half, half)], pl.ds(z * half, half)
                return [jnp.dot(lhs, wbuf[ws, q, depth], preferred_element_type=F32) for q in range(2)]

            gate, up = products_of(0)

            if nxt == 2:
                start(u_part(lax.rem(i + 2, nt), 0, ws))
            else:
                @when(i < nt - 2 + nxt)
                def _():
                    start(u_part(lax.rem(i + 2, nt), 0, ws))

            gate2, up2 = products_of(1)
            h = (jax.nn.silu(gate + gate2) * (up + up2)).astype(BF16)
            for q in range(2):
                h0[pl.ds(where[q], hr), u_cols(i)] = h[q * hr : (q + 1) * hr]
                hk[pl.ds(m + keep[q], hr), u_cols(i)] = h[(2 + q) * hr : (3 + q) * hr]
            return carry

        lax.fori_loop(0, nt, body, 0)
        h_push(h0, idx, parts - 1, keep, where, hr)

    def u_big(xb, slot, keep, where, idx, hook):
        def body(i, carry):
            ws = lax.rem(i, 2)
            hook(i)

            for part in range(parts - 1):
                @when(i == cuts[part + 1])
                def _():
                    h_push(h0, idx, part, keep, where, seg)

            start(u_copies(lax.rem(i + 1, nt), 1 - ws))

            @when(i == 0)
            def _():
                loaded(xb, slot, seg)

            wait(u_copies(i, ws))
            h = hidden(xb.at[slot], ws)
            for q in range(2):
                h0[pl.ds(where[q], seg), u_cols(i)] = h[q * seg : (q + 1) * seg]
                hk[pl.ds(m + keep[q], seg), u_cols(i)] = h[(2 + q) * seg : (3 + q) * seg]
            return carry

        lax.fori_loop(0, nt, body, 0)
        h_push(h0, idx, parts - 1, keep, where, seg)

    def sum_copy(hop, n, hf):
        part = pl.ds(hf * half_rows, half_rows)
        return remote(out.at[n, part], rs.at[hop, n, part], rs_s.at[n, hf], rs_r.at[hop, 2 * n + hf], (sp, sm)[hf])

    def in_copy(hop, n):
        b = lax.rem(n, 2)
        return pltpu.make_async_copy(rs.at[hop, n], inb.at[b], isem.at[b])

    def in_start(hop, n):
        for hf in range(2):
            sum_copy(hop, n, hf).wait_recv()
        in_copy(hop, n).start()

    def products(h, n, q):
        p, o = d_rows(q)
        ws = lax.rem(n, 2)
        cols = slice(q * tn, (q + 1) * tn)
        term = jnp.dot(h[...], wbuf[ws, p, pl.ds(o, 2 * hid)], preferred_element_type=F32)
        return term + inb[lax.rem(n, 2), :, cols].astype(F32), cols

    def land(n, i):
        return hk.at[pl.ds(pl.multiple_of(n * rows, rows), rows), pl.ds(i * dt, dt)]

    def a_copy(n, hf):
        return remote(out.at[n, pl.ds(hf * hr, hr)], land(n, 2).at[pl.ds(hf * hr, hr)], a_s.at[n, hf], a_r.at[n, hf], (fp, fm)[hf])

    def b_copy(n, i):
        return remote(out.at[n, pl.ds((1 + i) * rows, rows)], land(n, i), b_s.at[n, i], b_r.at[n, i], (fp, fm)[i])

    def y_copy(n):
        cols = pl.ds(pl.multiple_of(n * dt, dt), dt)
        return pltpu.make_async_copy(out.at[n, pl.ds(3 * rows, rows)], y.at[:, cols], ysem.at[n])

    def rounds(xb):
        start(u_copies(0, 0))
        start(u_part(1, 0, 1))
        for i in range(2):
            load_small(xb, 0, i, 0, 0, i)
        barrier = pltpu.get_barrier_semaphore()
        for dev in (fp, fm, sp, sm, sib):
            pl.semaphore_signal(barrier, 1, device_id={"tp": dev})
        pl.semaphore_wait(barrier, 5)

        for hf in range(2):
            hand(0, 0, hf).start()
        for hf in range(2):
            move(source(0, 0, hf), 0, 1, hf, fp).start()
            move(source(0, 0, hf), 0, 2, hf, fm).start()
        inb[...] = jnp.zeros_like(inb)
        for i in range(2, 4):
            load_small(xb, 0, i, 0, 0, i - 2)

        def on(i, v, *calls):
            @when(i == v)
            def _():
                for fn, *a in calls:
                    fn(*a)

        def hook(i):
            on(i, nt - 2, (arrive, 0, 1, 0), (arrive, 0, 2, 0), (load_mid, xb, 1, 0))

        u_small(xb, 0, (0, hr), (row0(0, 0), row0(0, 1)), 0, hook, True, 1)
        arrive(0, 1, 1)
        arrive(0, 2, 1)
        forward(0, 0)
        forward(0, 1)
        for i in range(1, 4):
            load_mid(xb, 1, i)

        def hook(i):
            @when(i < pieces // 3)
            def _():
                w_piece(i).start()

            on(i, 3, (push, 1, 0))
            on(i, 4, (forward, 0, 2))
            on(i, 5, (push, 1, 1), (load_pair, xb, 0, 0, 0, 1, 0, 0), (load_pair, xb, 0, 1, 0, 1, 0, 1))

        u_big(xb, 1, (seg, half_rows + seg), (row0(1, 0), row0(1, 1)), 1, hook)
        for hf in range(2):
            load_pair(xb, 0, 2 + hf, 1, 1, 0, hf)

        def one_round(k, carry):
            fi = 2 // (k + 1)
            first = k == 1

            def up(it, carry):
                b = fi * (it // nt) + (1 - fi) * lax.rem(it, 2)
                i = fi * lax.rem(it, nt) + (1 - fi) * (it // 2)
                ws = lax.rem(i, 2)

                @when(first)
                def _():
                    @when(it < pieces // 3)
                    def _():
                        w_piece(pieces // 3 + it).start()

                    @when((it > nt) & (it <= nt + pieces // 3))
                    def _():
                        w_piece(2 * (pieces // 3) + it - nt - 1).start()

                    def keep(c):
                        return (c * seg, half_rows + c * seg)

                    def where(c):
                        return (row0(2 * c, 0), row0(2 * c, 1))

                    on(it, 0, (h_sent, 0, hr))
                    on(it, 0, (far, 1, 0))
                    on(it, 1, (push, 1, 2), (far, 1, 1))
                    on(it, 4, (push, 1, 3), (forward, 1, 0))
                    on(it, 5, (load_pair, xb, 1, 0, 0, 1, 1, 0), (load_pair, xb, 1, 1, 0, 1, 1, 1),
                       (load_pair, xb, 1, 2, 1, 1, 1, 0), (load_pair, xb, 1, 3, 1, 1, 1, 1))
                    on(it, nt, (h_push, hk, 3, parts - 1, keep(0), where(0), seg), (h_sent, 1, seg), (forward, 1, 1))
                    on(it, 7, (forward, 1, 2))
                    on(it, 8, (forward, 1, 3))
                    on(it, 9, (push, 2, 0))
                    on(it, 11, (push, 2, 1))
                    for part in range(parts - 1):
                        for c in range(2):
                            on(it, c * nt + cuts[part + 1], (h_push, hk, 3 + c, part, keep(c), where(c), seg))

                @when(k > 1)
                def _():
                    on(it, 2 * nt - 2, (in_start, k - 2, 0))
                    for part in range(1, parts):
                        @when(it == 2 * nt - 3 + part)
                        def _():
                            hy_copy(part).start()

                @when(first & (it < 2 * nt - 1))
                def _():
                    start(u_copies(lax.rem(i + 1, nt), 1 - ws))

                @when(it == 2 * nt - 1)
                def _():
                    @when(first)
                    def _():
                        for q in range(pieces):
                            w_piece(q).wait_recv()

                    start(d_copies(0, 0))

                @when(first & (i == 0))
                def _():
                    loaded(xb, b, seg)

                @when(first | (b == 0))
                def _():
                    wait(u_copies(i, ws))

                h = hidden(xb.at[b], ws)
                for q in range(4):
                    r = fi * (q * half_rows + b * seg) + (1 - fi) * ((1 - b) * m + q * seg)
                    hk[pl.ds(pl.multiple_of(r, seg), seg), u_cols(i)] = h[q * seg : (q + 1) * seg]
                return carry

            def up_both(i, carry):
                ws = lax.rem(i, 2)
                start(u_copies(i + 1, 1 - ws))

                @when(k == 2)
                def _():
                    on(i, 0, (h_sent, 3, seg), (h_sent, 4, seg))
                    on(i, 2, (push, 3, 0))
                    on(i, 4, (push, 3, 1))

                @when(k == 3)
                def _():
                    on(i, 4, (push, 0, 3))

                    @when(i == 0)
                    def _():
                        for part in range(parts):
                            hy_copy(part).wait_send()

                @when(i == cuts[1])
                def _():
                    pl.semaphore_wait(hfree, 1)
                    hy_copy(0).start()

                @when(i == 0)
                def _():
                    for slot in range(2):
                        loaded(xb, slot, seg)

                wait(u_copies(i, ws))
                hk[pl.ds(m, m), u_cols(i)] = hidden(xb.at[0], ws)
                hk[pl.ds(0, m), u_cols(i)] = hidden(xb.at[1], ws)
                return carry

            lax.fori_loop(0, (1 - fi) * (nt - 1), up_both, 0)
            lax.fori_loop((1 - fi) * 2 * (nt - 1), 2 * nt, up, 0)

            @when(first)
            def _():
                h_push(hk, 4, parts - 1, (seg, half_rows + seg), (row0(2, 0), row0(2, 1)), seg)
                h_here(3, seg)
                h_here(4, seg)

            @when(k > 1)
            def _():
                for part in range(parts):
                    hy_copy(part).wait_recv()

            def down(n, carry):
                ws = lax.rem(n, 2)

                @when(n < nd - 1)
                def _():
                    start(d_copies(n + 1, 1 - ws))

                @when(n == nd - 1)
                def _():
                    start(u_copies(0, 0))

                @when(k > 1)
                def _():
                    in_copy(k - 2, n).wait()

                    @when(n < nd - 1)
                    def _():
                        in_start(k - 2, n + 1)

                    for hf in range(2):
                        sum_copy(0, n, hf).wait_send()

                @when(first)
                def _():
                    on(n, 0, (forward, 2, 0))
                    on(n, 1, (push, 2, 2))
                    on(n, 2, (forward, 2, 1))
                    on(n, 4, (push, 2, 3))
                    on(n, 5, (forward, 2, 2))
                    on(n, 7, (forward, 2, 3))

                @when(k == 2)
                def _():
                    on(n, 2, (push, 3, 2))
                    on(n, 4, (push, 3, 3))
                    on(n, 7, (far, 0, 0), (far, 0, 1))

                @when(k < 3)
                def _():
                    for v, other, pair in ((1, 0, 0), (3, 1, 0), (5, 0, 1), (6, 1, 1)):
                        @when(n == v)
                        def _():
                            for hf in range(2):
                                load_pair(xb, 1 - other, 2 * hf + pair, other, k + 1, pair, hf)

                @when(k == 3)
                def _():
                    for q in range(4):
                        on(n, 2 + q, (load_small, xb, 0, q, 0, 3, q % 2))

                wait(d_copies(n, ws))
                for q in range(sub):
                    total, cols = products(hk.at[pl.ds(0, m)], n, q)
                    out[n, :, cols] = total.astype(BF16)
                for hf in range(2):
                    sum_copy(k - 1, n, hf).start()
                return carry

            lax.fori_loop(0, nd, down, 0)

            @when(k < 3)
            def _():
                pl.semaphore_signal(hfree, 1, device_id={"tp": sib})

            return carry

        lax.fori_loop(1, side, one_round, 0)

        def hook(i):
            on(i, nt - 2, (in_start, 2, 0))

        for part in range(parts):
            hy_copy(part).wait_send()
        u_small(xb, 0, (0, hr), (row0(3, 0), row0(3, 1)), 5, hook, False, 0)

    pl.run_scoped(rounds, pltpu.VMEM((2, 8 * hr, d), BF16))

    def last(t0, t1, t2):
        h_sent(5, hr)
        for dev in (fp, fm):
            pl.semaphore_signal(nfree, 1, device_id={"tp": dev})
        for idx, size in ((0, hr), (1, seg), (5, hr)):
            h_here(idx, size)

        def add_far(n):
            for hf in range(2):
                a_copy(n, hf).wait_recv()
            far_in = land(n, 2)[...].astype(F32)
            out[n, pl.ds(rows, hr)] = (t2[n, :hr] + far_in[:hr]).astype(BF16)
            out[n, pl.ds(rows + hr, hr)] = t2[n, hr:].astype(BF16)
            out[n, pl.ds(2 * rows, hr)] = t1[n, :hr].astype(BF16)
            out[n, pl.ds(2 * rows + hr, hr)] = (t1[n, hr:] + far_in[hr:]).astype(BF16)
            for i in range(2):
                b_copy(n, i).start()

        def add_near(n):
            for i in range(2):
                b_copy(n, i).wait_recv()
            out[n, pl.ds(3 * rows, rows)] = (t0[n] + land(n, 0)[...].astype(F32) + land(n, 1)[...].astype(F32)).astype(BF16)
            y_copy(n).start()

        def down(n, carry):
            ws = lax.rem(n, 2)

            @when(n < nd - 1)
            def _():
                start(d_copies(n + 1, 1 - ws))

            in_copy(2, n).wait()

            @when(n < nd - 1)
            def _():
                in_start(2, n + 1)

            for hf in range(2):
                sum_copy(0, n, hf).wait_send()

            @when(n >= 2)
            def _():
                add_far(n - 2)

            @when(n >= 4)
            def _():
                add_near(n - 4)

            wait(d_copies(n, ws))
            for q in range(sub):
                total, cols = products(h0, n, q)
                for hf in range(2):
                    o = hf * half_rows
                    dst = pl.ds(hf * hr, hr)
                    t0[n, dst, cols] = total[o : o + hr]
                    t1[n, dst, cols] = total[o + hr : o + 2 * hr]
                    t2[n, dst, cols] = total[o + 2 * hr : o + 3 * hr]
                    out[n, dst, cols] = total[o + 3 * hr : o + 4 * hr].astype(BF16)
            @when(n == 0)
            def _():
                pl.semaphore_wait(nfree, 2)

            for hf in range(2):
                a_copy(n, hf).start()
            return carry

        lax.fori_loop(0, nd, down, 0)
        add_far(nd - 2)
        add_near(nd - 4)
        add_far(nd - 1)
        for n in range(nd - 3, nd):
            add_near(n)

    shape = pltpu.VMEM((nd, rows, dt), F32)
    pl.run_scoped(last, shape, shape, shape)

    for n in range(nd):
        y_copy(n).wait()
        for i in range(2):
            a_copy(n, i).wait_send()
            b_copy(n, i).wait_send()
    for i in range(pieces):
        w_piece(i).wait_send()
    for k in range(side):
        for j in range(side):
            for hf in range(2):
                hand(k, j, hf).wait_send()
                if k or j:
                    move(piece(k, j, hf), k, j, hf, sib).wait_send()


def build(mesh, tn, dt):
    side = math.isqrt(mesh.shape["tp"] // 2)

    def step(x, w_gate, w_up, w_down):
        rows, d = x.shape
        hid = w_gate.shape[1]
        hr = rows // 2
        nt, nd = hid // tn, d // dt
        dma = pltpu.SemaphoreType.DMA
        hbm = pl.BlockSpec(memory_space=pltpu.HBM)
        m = side * rows
        result = pl.pallas_call(
            functools.partial(kernel, side, tn, dt),
            out_shape=(
                jax.ShapeDtypeStruct((rows, d), BF16),
                jax.ShapeDtypeStruct((2, side, m, d), BF16),
                jax.ShapeDtypeStruct((hid, d), BF16),
                jax.ShapeDtypeStruct((side - 1, nd, m, dt), BF16),
            ),
            in_specs=[hbm] * 4,
            out_specs=[hbm] * 4,
            scratch_shapes=[
                pltpu.VMEM((2, 2, d, tn), BF16),
                pltpu.VMEM((m, 2 * hid), BF16),
                pltpu.VMEM((2 * m, 2 * hid), BF16),
                pltpu.VMEM((nd, m, dt), BF16),
                pltpu.VMEM((2, m, dt), BF16),
                dma((2, 2 * dt // tn)),
                dma((2, 4)),
                dma((2,)),
                dma((nd,)),
                dma((side, 2 * side)),
                dma((side, 2 * side)),
                dma((side, 2 * side)),
                dma((side, 2 * side)),
                dma((12,)),
                dma((12,)),
                dma((6, 6)),
                dma((6, 6)),
                dma((3,)),
                dma((3,)),
                dma((nd, 2)),
                dma((side - 1, 2 * nd)),
                dma((nd, 2)),
                dma((nd, 2)),
                dma((nd, 2)),
                dma((nd, 2)),
                pltpu.SemaphoreType.REGULAR,
                pltpu.SemaphoreType.REGULAR,
            ],
            compiler_params=pltpu.CompilerParams(collective_id=0, has_side_effects=True, vmem_limit_bytes=67043328),
            cost_estimate=pl.CostEstimate(flops=6 * side * side * 2 * rows * d * hid, bytes_accessed=9 * d * hid * 4, transcendentals=0),
            name="mlp",
        )(x, w_gate, w_up, w_down)
        return result[0]

    return jax.shard_map(
        step,
        mesh=mesh,
        in_specs=(P(("dp", "tp"), None), P(None, "tp"), P(None, "tp"), P("tp", None)),
        out_specs=P(("dp", "tp"), None),
        check_vma=False,
    )


def solution(mesh):
    return build(mesh, 256, 1024)
```

time: 412 us -> 389 us (0.944)
  Pallas kernels: 408 us -> 386 us
    pallas_call x1, Pallas kernels: 408 us -> 386 us  [step(): pl.pallas_call(functools.partial(kernel, side, tn, dt), out_shape=(jax.Sh...]
where the time goes in v2:
time: 389 us
  Pallas kernels  386 us (99%)
    pallas_call x1, Pallas kernels, step(): pl.pallas_call(functools.partial(kernel, side, tn, dt), out_shape=(jax.Sh...  386 us

profile of v2, /device:TPU:97, one launch (start us, length us, event | category | flops | bytes accessed | tf_op | source)
XLA Modules:
  0.0 388.6 jit_solution(15296668427445873586)
XLA Ops:
  0.0 385.5 %mlp.1 = (bf16[128,8192]{1,0:T(8,128)(2,1)}, bf16[2,4,512,8192]{3,2,1,0:T(8,128)(2,1)}, bf16[1536,8192]{1,0:T(8,128)(2,1)}, bf16[3,8,512,1024]{3,2,1,0:T(8,128)(2,1)}) custom-call(bf16[128,8192]{1,0:T(8,128)(2,1)} %x.1, bf16[8192,1536]{1,0:T(8,128)(2,1)} %wg.1, bf16[8192,1536]{1,0:T(8,128)(2,1)} %wu.1, bf16[1536,8192]{1,0:T(8,128)(2,1)} %wd.1), custom_call_target="tpu_custom_call" | custom-call | flops 309237645312 | bytes 452984832 | tf_op jit(solution)/shard_map/mlp/pallas_call | solution.py:644
  385.5 3.1 copy.6

commit v3 on v2

v3 whole, which is shorter than its diff:
```python
import functools
import math

import jax
import jax.numpy as jnp
from jax import lax
from jax.experimental import pallas as pl
from jax.experimental.pallas import tpu as pltpu
from jax.sharding import PartitionSpec as P

F32, BF16 = jnp.float32, jnp.bfloat16


def kernel(side, tn, dt, x, wg, wu, wd, y, xs, wp, rs, wbuf, h0, hk, out, inb, wsem, xsem, isem, ysem,
           ag_s, ag_r, pu_s, pu_r, wp_s, wp_r, hx_s, hx_r, hy_s, hy_r, rs_s, rs_r, a_s, a_r, b_s, b_r, hfree, nfree):
    rows, d = x.shape
    hid = wg.shape[1]
    hr = rows // 2
    half_rows = side * hr
    m = 2 * half_rows
    seg = 2 * hr
    nt, nd = hid // tn, d // dt
    sub = dt // tn
    cuts = (0, nt // 3, nt - 1, nt)
    parts = len(cuts) - 1
    pieces = 2 * nt
    dt2, ne = dt // 2, 2 * nd

    t = lax.axis_index("tp")
    c = lax.rem(t, 2)
    cx, cy = t // (2 * side), lax.rem(t // 2, side)
    f, s = cx * (1 - c) + cy * c, cy * (1 - c) + cx * c

    def at(df, ds):
        ff, ss = lax.rem(f + df + side, side), lax.rem(s + ds + side, side)
        return ((ff * (1 - c) + ss * c) * side + ss * (1 - c) + ff * c) * 2 + c

    fp, fm, sp, sm, sib = at(1, 0), at(-1, 0), at(0, 1), at(0, -1), t + 1 - 2 * c

    def remote(src, dst, send, recv, dev):
        return pltpu.make_async_remote_copy(src_ref=src, dst_ref=dst, send_sem=send, recv_sem=recv, device_id={"tp": dev})

    def when(cond):
        return pl.when(cond)

    def row0(j, hf):
        return hf * half_rows + j * hr

    def piece(k, j, hf, other=0):
        return xs.at[other, k, pl.ds(row0(j, hf), hr)]

    def source(k, j, hf):
        if isinstance(k, int) and isinstance(j, int) and k == 0 and j == 0:
            return x.at[pl.ds(hf * hr, hr)]
        return piece(k, j, hf)

    def move(src, k, j, hf, dev):
        i = j * 2 + hf
        return remote(src, piece(k, j, hf), ag_s, ag_r.at[k, i], dev)

    def hand(k, j, hf):
        i = j * 2 + hf
        return remote(source(k, j, hf), piece(k, j, hf, 1), pu_s, pu_r.at[k, i], sib)

    def arrive(k, j, hf):
        move(piece(k, j, hf), k, j, hf, sib).wait_recv()
        hand(k, j, hf).start()

    def push(k, j):
        for hf in range(2):
            arrive(k, j, hf)

    def forward(k, j):
        for hf, dev in ((0, sp), (1, sm)):
            move(source(k, j, hf), k + 1, j, hf, dev).start()

    def far(k, hf):
        move(piece(k, 1 + hf, hf), k, 3, hf, (fp, fm)[hf]).start()

    def load(xb, slot, row, src, size, sem):
        pltpu.make_async_copy(src, xb.at[slot, pl.ds(row, size)], xsem.at[sem]).start()

    def loaded(xb, slot, row, size, sem):
        dst = xb.at[slot, pl.ds(row, size)]
        pltpu.make_async_copy(dst, dst, xsem.at[sem]).wait()

    def load_small(xb, i, k, j, hf):
        if i < 2:
            src = source(k, j, hf)
        else:
            hand(k, j, hf).wait_recv()
            src = piece(k, j, hf, 1)
        load(xb, 0, i * hr, src, hr, 0)

    def load_mid(xb, other, hf):
        if other:
            for j in (1, 2):
                hand(0, j, hf).wait_recv()
        load(xb, 1, (2 * hf + other) * seg, xs.at[other, 0, pl.ds(row0(1, hf), seg)], seg, 1 + hf)

    def load_pair(xb, slot, i, other, k, pair, hf):
        for q in range(2):
            @when(other == 1)
            def _():
                hand(k, 2 * pair + q, hf).wait_recv()
        load(xb, slot, i * seg, xs.at[other, k, pl.ds(hf * half_rows + pair * seg, seg)], seg, slot)

    def u_part(n, z, slot):
        cols, depth = pl.ds(pl.multiple_of(n * tn, tn), tn), pl.ds(z * (d // 2), d // 2)
        return [pltpu.make_async_copy(w.at[depth, cols], wbuf.at[slot, i, depth], wsem.at[slot, z]) for i, w in enumerate((wg, wu))]

    def u_copies(n, slot):
        return u_part(n, 0, slot) + u_part(n, 1, slot)

    def d_rows(q):
        return q // 2, (q % 2) * 2 * hid

    def d_copies(n, slot):
        r = []
        for q in range(sub):
            p, o = d_rows(q)
            cols = pl.ds(pl.multiple_of(n * dt + q * tn, tn), tn)
            for i, w in enumerate((wd, wp)):
                r.append(pltpu.make_async_copy(w.at[:, cols], wbuf.at[slot, p, pl.ds(o + i * hid, hid)], wsem.at[slot, 0]))
        return r

    def start(copies):
        for cp in copies:
            cp.start()

    def held(slot, z, depth):
        dst = wbuf.at[slot, :, depth]
        pltpu.make_async_copy(dst, dst, wsem.at[slot, z]).wait()

    def u_held(z, slot):
        held(slot, z, pl.ds(z * (d // 2), d // 2))

    def d_held(slot):
        held(slot, 0, pl.ds(0, sub * hid))

    def cut(part):
        return cuts[part] * tn, (cuts[part + 1] - cuts[part]) * tn

    def h_copy(hdst, idx, part, src, dst, size):
        lo, width = cut(part)
        return remote(hk.at[pl.ds(m + src, size), pl.ds(lo, width)], hdst.at[pl.ds(dst, size), pl.ds(hid + lo, width)],
                      hx_s.at[idx], hx_r.at[idx], sib)

    def h_push(hdst, idx, part, src, dst, size):
        for q in range(2):
            h_copy(hdst, idx, part, src[q], dst[q], size).start()

    def h_all(idx, size):
        r = pl.ds(0, 2 * size)
        return remote(hk.at[r, pl.ds(0, hid)], hk.at[r, pl.ds(hid, hid)], hx_s.at[idx], hx_r.at[idx], sib)

    def h_sent(idx, size):
        h_all(idx, size).wait_send()

    def h_here(idx, size):
        h_all(idx, size).wait_recv()

    def hy_copy(lo, size):
        return remote(hk.at[pl.ds(m, m), pl.ds(lo, size)], hk.at[pl.ds(0, m), pl.ds(hid + lo, size)], hy_s, hy_r, sib)

    def hy_all():
        return hy_copy(0, hid)

    def w_piece(i):
        r = pl.ds(i * (hid // pieces), hid // pieces)
        return remote(wd.at[r], wp.at[r], wp_s, wp_r, sib)

    def hidden(lhs, ws):
        gate = jnp.dot(lhs[...], wbuf[ws, 0], preferred_element_type=F32)
        up = jnp.dot(lhs[...], wbuf[ws, 1], preferred_element_type=F32)
        return (jax.nn.silu(gate) * up).astype(BF16)

    def u_cols(i):
        return pl.ds(pl.multiple_of(i * tn, tn), tn)

    def u_small(xb, slot, row, sem, keep, where, idx, hook, end, ahead, nxt):
        half = d // 2

        def after(i, more):
            return lax.rem(i + more, end) if nxt == 2 else i + more

        def body(i, carry):
            ws = lax.rem(i, 2)
            hook(i)

            for part in range(parts):
                if cuts[part + 1] < end:
                    @when(i == cuts[part + 1])
                    def _():
                        h_push(h0, idx, part, keep, where, hr)

            if not ahead:
                @when(i == 0)
                def _():
                    start(u_part(1, 0, 1))

            if nxt:
                start(u_part(after(i, 1), 1, 1 - ws))
            else:
                @when(i < end - 1)
                def _():
                    start(u_part(i + 1, 1, 1 - ws))

                @when(i == end - 1)
                def _():
                    start(d_copies(0, 0))

            @when(i == 0)
            def _():
                loaded(xb, slot, row, 4 * hr, sem)

            def products_of(z):
                u_held(z, ws)
                depth = pl.ds(z * half, half)
                lhs = xb[slot, pl.ds(row, 4 * hr), depth]
                return [jnp.dot(lhs, wbuf[ws, q, depth], preferred_element_type=F32) for q in range(2)]

            gate, up = products_of(0)

            if nxt == 2:
                start(u_part(after(i, 2), 0, ws))
            else:
                @when(i < end - 2 + nxt)
                def _():
                    start(u_part(i + 2, 0, ws))

            gate2, up2 = products_of(1)
            h = (jax.nn.silu(gate + gate2) * (up + up2)).astype(BF16)
            for q in range(2):
                h0[pl.ds(where[q], hr), u_cols(i)] = h[q * hr : (q + 1) * hr]
                hk[pl.ds(m + keep[q], hr), u_cols(i)] = h[(2 + q) * hr : (3 + q) * hr]
            return carry

        lax.fori_loop(0, end, body, 0)
        for part in range(parts):
            if cuts[part + 1] == end:
                h_push(h0, idx, part, keep, where, hr)

    def u_big(xb, keep, where, idx, hook, begin):
        def body(i, carry):
            ws = lax.rem(i, 2)
            hook(i)

            for part in range(1, parts - 1):
                @when(i == cuts[part + 1])
                def _():
                    h_push(h0, idx, part, keep, where, seg)

            start(u_copies(lax.rem(i + 1, nt), 1 - ws))
            u_held(0, ws)
            u_held(1, ws)
            h = hidden(xb.at[1], ws)
            for q in range(2):
                h0[pl.ds(where[q], seg), u_cols(i)] = h[2 * q * seg : (2 * q + 1) * seg]
                hk[pl.ds(m + keep[q], seg), u_cols(i)] = h[(2 * q + 1) * seg : (2 * q + 2) * seg]
            return carry

        lax.fori_loop(begin, nt, body, 0)
        h_push(h0, idx, parts - 1, keep, where, seg)

    def sum_copy(hop, n, hf):
        part = pl.ds(hf * half_rows, half_rows)
        return remote(out.at[n, part], rs.at[hop, n, part], rs_s.at[n], rs_r.at[hop, n], (sp, sm)[hf])

    def sum_all(hop, n):
        return remote(out.at[n], rs.at[hop, n], rs_s.at[n], rs_r.at[hop, n], sp)

    def in_copy(hop, n):
        b = lax.rem(n, 2)
        return pltpu.make_async_copy(rs.at[hop, n], inb.at[b], isem.at[b])

    def in_start(hop, n):
        sum_all(hop, n).wait_recv()
        in_copy(hop, n).start()

    def products(h, n, q):
        p, o = d_rows(q)
        ws = lax.rem(n, 2)
        cols = slice(q * tn, (q + 1) * tn)
        term = jnp.dot(h[...], wbuf[ws, p, pl.ds(o, 2 * hid)], preferred_element_type=F32)
        return term + inb[lax.rem(n, 2), :, cols].astype(F32), cols

    def step_cols(e, base=0):
        return pl.ds(pl.multiple_of(base + lax.rem(e, 2) * dt2, dt2), dt2)

    def land(e, i):
        r = pl.ds(pl.multiple_of((e // 2) * rows, rows), rows)
        return hk.at[r, step_cols(e, i * dt)]

    def leave(e, row, size):
        return out.at[e // 2, pl.ds(row, size), step_cols(e)]

    def a_copy(e, hf):
        return remote(leave(e, hf * hr, hr), land(e, 2).at[pl.ds(hf * hr, hr)], a_s, a_r.at[e], (fp, fm)[hf])

    def b_copy(e, i):
        return remote(leave(e, (1 + i) * rows, rows), land(e, i), b_s, b_r.at[e], (fp, fm)[i])

    def y_copy(e):
        cols = pl.ds(pl.multiple_of(e * dt2, dt2), dt2)
        return pltpu.make_async_copy(leave(e, 3 * rows, rows), y.at[:, cols], ysem)

    def rounds(xb):
        start(u_copies(0, 0))
        start(u_part(1, 0, 1))
        for i in range(2):
            load_small(xb, i, 0, 0, i)
        barrier = pltpu.get_barrier_semaphore()
        for dev in (fp, fm, sp, sm, sib):
            pl.semaphore_signal(barrier, 1, device_id={"tp": dev})
        pl.semaphore_wait(barrier, 5)

        for hf in range(2):
            hand(0, 0, hf).start()
        for hf in range(2):
            move(source(0, 0, hf), 0, 1, hf, fp).start()
            move(source(0, 0, hf), 0, 2, hf, fm).start()
        inb[...] = jnp.zeros_like(inb)
        for i in range(2, 4):
            load_small(xb, i, 0, 0, i - 2)

        def on(i, v, *calls):
            @when(i == v)
            def _():
                for fn, *a in calls:
                    fn(*a)

        def hook(i):
            on(i, nt - 3, (arrive, 0, 1, 0), (arrive, 0, 2, 0), (load_mid, xb, 0, 0))
            on(i, nt - 1, (load_mid, xb, 1, 0))

        u_small(xb, 0, 0, 0, (0, hr), (row0(0, 0), row0(0, 1)), 0, hook, nt, True, 2)

        def hook(i):
            on(i, 0, (forward, 0, 0))
            on(i, 1, (arrive, 0, 1, 1), (arrive, 0, 2, 1), (forward, 0, 1), (load_mid, xb, 0, 1))

        u_small(xb, 1, 0, 1, (seg, seg + hr), (row0(1, 0), row0(2, 0)), 1, hook, cuts[1], True, 2)
        load_mid(xb, 1, 1)

        def hook(i):
            pass

        u_small(xb, 1, 2 * seg, 2, (half_rows + seg, half_rows + seg + hr), (row0(1, 1), row0(2, 1)), 1, hook, cuts[1], True, 1)

        def hook(i):
            @when(i < cuts[1] + 2)
            def _():
                for q in range(2):
                    w_piece(2 * (i - cuts[1]) + q).start()

            on(i, nt - 2, (forward, 0, 2), (push, 1, 0))
            on(i, nt - 1, (push, 1, 1), (load_pair, xb, 0, 0, 0, 1, 0, 0), (load_pair, xb, 0, 1, 0, 1, 0, 1))

        u_big(xb, (seg, half_rows + seg), (row0(1, 0), row0(1, 1)), 1, hook, cuts[1])
        for hf in range(2):
            load_pair(xb, 0, 2 + hf, 1, 1, 0, hf)

        def one_round(k, carry):
            fi = 2 // (k + 1)
            first = k == 1

            def up(it, carry):
                b = fi * (it // nt) + (1 - fi) * lax.rem(it, 2)
                i = fi * lax.rem(it, nt) + (1 - fi) * (it // 2)
                ws = lax.rem(i, 2)

                @when(first)
                def _():
                    @when(it < pieces // 3)
                    def _():
                        w_piece(pieces // 3 + it).start()

                    @when((it > nt) & (it <= nt + pieces // 3))
                    def _():
                        w_piece(2 * (pieces // 3) + it - nt - 1).start()

                    def keep(c):
                        return (c * seg, half_rows + c * seg)

                    def where(c):
                        return (row0(2 * c, 0), row0(2 * c, 1))

                    on(it, 0, (h_sent, 0, hr))
                    on(it, 0, (far, 1, 0))
                    on(it, 1, (push, 1, 2), (far, 1, 1))
                    on(it, 4, (push, 1, 3), (forward, 1, 0))
                    on(it, 5, (load_pair, xb, 1, 0, 0, 1, 1, 0), (load_pair, xb, 1, 1, 0, 1, 1, 1),
                       (load_pair, xb, 1, 2, 1, 1, 1, 0), (load_pair, xb, 1, 3, 1, 1, 1, 1))
                    on(it, nt, (h_push, hk, 3, parts - 1, keep(0), where(0), seg), (h_sent, 1, seg), (forward, 1, 1))
                    on(it, 7, (forward, 1, 2))
                    on(it, 8, (forward, 1, 3))
                    on(it, 9, (push, 2, 0))
                    on(it, 11, (push, 2, 1))
                    for part in range(parts - 1):
                        for c in range(2):
                            on(it, c * nt + cuts[part + 1], (h_push, hk, 3 + c, part, keep(c), where(c), seg))

                @when(k > 1)
                def _():
                    on(it, 2 * nt - 2, (in_start, k - 2, 0))
                    for part in range(1, parts):
                        @when(it == 2 * nt - 3 + part)
                        def _():
                            hy_copy(*cut(part)).start()

                @when(first & (it < 2 * nt - 1))
                def _():
                    start(u_copies(lax.rem(i + 1, nt), 1 - ws))

                @when(it == 2 * nt - 1)
                def _():
                    @when(first)
                    def _():
                        remote(wd, wp, wp_s, wp_r, sib).wait_recv()

                    start(d_copies(0, 0))

                @when(first & (i == 0))
                def _():
                    loaded(xb, b, 0, 4 * seg, b)

                @when(first | (b == 0))
                def _():
                    u_held(0, ws)
                    u_held(1, ws)

                h = hidden(xb.at[b], ws)
                for q in range(4):
                    r = fi * (q * half_rows + b * seg) + (1 - fi) * ((1 - b) * m + q * seg)
                    hk[pl.ds(pl.multiple_of(r, seg), seg), u_cols(i)] = h[q * seg : (q + 1) * seg]
                return carry

            def up_both(i, carry):
                ws = lax.rem(i, 2)
                start(u_copies(i + 1, 1 - ws))

                @when(k == 2)
                def _():
                    on(i, 0, (h_sent, 3, seg), (h_sent, 4, seg))
                    on(i, 2, (push, 3, 0))
                    on(i, 4, (push, 3, 1))

                @when(k == 3)
                def _():
                    on(i, 4, (push, 0, 3))

                    @when(i == 0)
                    def _():
                        hy_all().wait_send()

                @when(i == cuts[1])
                def _():
                    pl.semaphore_wait(hfree, 1)
                    hy_copy(*cut(0)).start()

                @when(i == 0)
                def _():
                    for slot in range(2):
                        loaded(xb, slot, 0, 4 * seg, slot)

                u_held(0, ws)
                u_held(1, ws)
                hk[pl.ds(m, m), u_cols(i)] = hidden(xb.at[0], ws)
                hk[pl.ds(0, m), u_cols(i)] = hidden(xb.at[1], ws)
                return carry

            lax.fori_loop(0, (1 - fi) * (nt - 1), up_both, 0)
            lax.fori_loop((1 - fi) * 2 * (nt - 1), 2 * nt, up, 0)

            @when(first)
            def _():
                h_push(hk, 4, parts - 1, (seg, half_rows + seg), (row0(2, 0), row0(2, 1)), seg)
                h_here(3, seg)
                h_here(4, seg)

            @when(k > 1)
            def _():
                hy_all().wait_recv()

            def down(n, carry):
                ws = lax.rem(n, 2)

                @when(n < nd - 1)
                def _():
                    start(d_copies(n + 1, 1 - ws))

                @when(n == nd - 1)
                def _():
                    start(u_copies(0, 0))

                @when(k > 1)
                def _():
                    in_copy(k - 2, n).wait()

                    @when(n < nd - 1)
                    def _():
                        in_start(k - 2, n + 1)

                    sum_all(0, n).wait_send()

                @when(first)
                def _():
                    on(n, 0, (forward, 2, 0))
                    on(n, 1, (push, 2, 2))
                    on(n, 2, (forward, 2, 1))
                    on(n, 4, (push, 2, 3))
                    on(n, 5, (forward, 2, 2))
                    on(n, 7, (forward, 2, 3))

                @when(k == 2)
                def _():
                    on(n, 2, (push, 3, 2))
                    on(n, 4, (push, 3, 3))
                    on(n, 7, (far, 0, 0), (far, 0, 1))

                @when(k < 3)
                def _():
                    for v, other, pair in ((1, 0, 0), (3, 1, 0), (5, 0, 1), (6, 1, 1)):
                        @when(n == v)
                        def _():
                            for hf in range(2):
                                load_pair(xb, 1 - other, 2 * hf + pair, other, k + 1, pair, hf)

                @when(k == 3)
                def _():
                    for q in range(4):
                        on(n, 2 + q, (load_small, xb, q, 0, 3, q % 2))

                d_held(ws)
                for q in range(sub):
                    total, cols = products(hk.at[pl.ds(0, m)], n, q)
                    out[n, :, cols] = total.astype(BF16)
                for hf in range(2):
                    sum_copy(k - 1, n, hf).start()
                return carry

            lax.fori_loop(0, nd, down, 0)

            @when(k < 3)
            def _():
                pl.semaphore_signal(hfree, 1, device_id={"tp": sib})

            return carry

        lax.fori_loop(1, side, one_round, 0)

        def hook(i):
            on(i, nt - 2, (in_start, 2, 0))

        hy_all().wait_send()
        u_small(xb, 0, 0, 0, (0, hr), (row0(3, 0), row0(3, 1)), 5, hook, nt, False, 0)

    pl.run_scoped(rounds, pltpu.VMEM((2, 8 * hr, d), BF16))

    def last(t0, t1, t2):
        h_sent(5, hr)
        for dev in (fp, fm):
            pl.semaphore_signal(nfree, 1, device_id={"tp": dev})
        for idx, size in ((0, hr), (1, seg), (5, hr)):
            h_here(idx, size)

        def add_far(e):
            both = pl.ds(0, rows)
            remote(out.at[0, both, pl.ds(0, dt2)], land(e, 2), a_s, a_r.at[e], fp).wait_recv()
            far_in = land(e, 2)[...].astype(F32)
            leave(e, rows, hr)[...] = (t2[e, :hr] + far_in[:hr]).astype(BF16)
            leave(e, rows + hr, hr)[...] = t2[e, hr:].astype(BF16)
            leave(e, 2 * rows, hr)[...] = t1[e, :hr].astype(BF16)
            leave(e, 2 * rows + hr, hr)[...] = (t1[e, hr:] + far_in[hr:]).astype(BF16)
            for i in range(2):
                b_copy(e, i).start()

        def add_near(e):
            both = pl.ds(0, 2 * rows)
            remote(out.at[0, both, pl.ds(0, dt2)], out.at[0, both, pl.ds(0, dt2)], b_s, b_r.at[e], fp).wait_recv()
            leave(e, 3 * rows, rows)[...] = (t0[e] + land(e, 0)[...].astype(F32) + land(e, 1)[...].astype(F32)).astype(BF16)
            y_copy(e).start()

        def down(e, carry):
            n, c2 = e // 2, lax.rem(e, 2)
            ws = lax.rem(n, 2)

            @when(c2 == 0)
            def _():
                @when(n < nd - 1)
                def _():
                    start(d_copies(n + 1, 1 - ws))

                in_copy(2, n).wait()

                @when(n < nd - 1)
                def _():
                    in_start(2, n + 1)

                sum_all(0, n).wait_send()
                d_held(ws)

            @when(e >= 3)
            def _():
                add_far(e - 3)

            @when(e >= 6)
            def _():
                add_near(e - 6)

            for q in range(2):
                term = jnp.dot(h0[...], wbuf[ws, c2, pl.ds(q * 2 * hid, 2 * hid)], preferred_element_type=F32)
                cols = slice(q * tn, (q + 1) * tn)
                total = term + inb[lax.rem(n, 2), :, pl.ds(pl.multiple_of(c2 * dt2 + q * tn, tn), tn)].astype(F32)
                for hf in range(2):
                    o = hf * half_rows
                    dst = pl.ds(hf * hr, hr)
                    t0[e, dst, cols] = total[o : o + hr]
                    t1[e, dst, cols] = total[o + hr : o + 2 * hr]
                    t2[e, dst, cols] = total[o + 2 * hr : o + 3 * hr]
                    out[n, dst, pl.ds(pl.multiple_of(c2 * dt2 + q * tn, tn), tn)] = total[o + 3 * hr : o + 4 * hr].astype(BF16)

            @when(e == 0)
            def _():
                pl.semaphore_wait(nfree, 2)

            for hf in range(2):
                a_copy(e, hf).start()
            return carry

        lax.fori_loop(0, ne, down, 0)
        for i in range(3):
            add_near(ne - 6 + i)
            add_far(ne - 3 + i)
        for i in range(3):
            add_near(ne - 3 + i)

    shape = pltpu.VMEM((ne, rows, dt2), F32)
    pl.run_scoped(last, shape, shape, shape)

    pltpu.make_async_copy(y, y, ysem).wait()
    for sem, r in ((a_s, pl.ds(0, rows)), (b_s, pl.ds(rows, 2 * rows))):
        remote(out.at[:, r], out.at[:, r], sem, a_r.at[0], fp).wait_send()
    remote(wd, wp, wp_s, wp_r, sib).wait_send()
    remote(xs.at[1], xs.at[1], pu_s, pu_r.at[0, 0], sib).wait_send()
    sent = xs.at[0, :, pl.ds(0, 2 * (side * side - 1) * hr // side)]
    remote(sent, sent, ag_s, ag_r.at[0, 2], fp).wait_send()


def build(mesh, tn, dt):
    side = math.isqrt(mesh.shape["tp"] // 2)

    def step(x, w_gate, w_up, w_down):
        rows, d = x.shape
        hid = w_gate.shape[1]
        hr = rows // 2
        nt, nd = hid // tn, d // dt
        dma = pltpu.SemaphoreType.DMA
        hbm = pl.BlockSpec(memory_space=pltpu.HBM)
        m = side * rows
        result = pl.pallas_call(
            functools.partial(kernel, side, tn, dt),
            out_shape=(
                jax.ShapeDtypeStruct((rows, d), BF16),
                jax.ShapeDtypeStruct((2, side, m, d), BF16),
                jax.ShapeDtypeStruct((hid, d), BF16),
                jax.ShapeDtypeStruct((side - 1, nd, m, dt), BF16),
            ),
            in_specs=[hbm] * 4,
            out_specs=[hbm] * 4,
            scratch_shapes=[
                pltpu.VMEM((2, 2, d, tn), BF16),
                pltpu.VMEM((m, 2 * hid), BF16),
                pltpu.VMEM((2 * m, 2 * hid), BF16),
                pltpu.VMEM((nd, m, dt), BF16),
                pltpu.VMEM((2, m, dt), BF16),
                dma((2, 2)),
                dma((3,)),
                dma((2,)),
                dma,
                dma,
                dma((side, 2 * side)),
                dma,
                dma((side, 2 * side)),
                dma,
                dma,
                dma((6,)),
                dma((6,)),
                dma,
                dma,
                dma((nd,)),
                dma((side - 1, nd)),
                dma,
                dma((2 * nd,)),
                dma,
                dma((2 * nd,)),
                pltpu.SemaphoreType.REGULAR,
                pltpu.SemaphoreType.REGULAR,
            ],
            compiler_params=pltpu.CompilerParams(collective_id=0, has_side_effects=True, vmem_limit_bytes=67043328),
            cost_estimate=pl.CostEstimate(flops=6 * side * side * 2 * rows * d * hid, bytes_accessed=9 * d * hid * 4, transcendentals=0),
            name="mlp",
        )(x, w_gate, w_up, w_down)
        return result[0]

    return jax.shard_map(
        step,
        mesh=mesh,
        in_specs=(P(("dp", "tp"), None), P(None, "tp"), P(None, "tp"), P("tp", None)),
        out_specs=P(("dp", "tp"), None),
        check_vma=False,
    )


def solution(mesh):
    return build(mesh, 256, 1024)
```

time: 389 us -> 381 us (0.979)
  Pallas kernels: 386 us -> 378 us
    pallas_call x1, Pallas kernels: 386 us -> 378 us  [step(): pl.pallas_call(functools.partial(kernel, side, tn, dt), out_shape=(jax.Sh...]
where the time goes in v3:
time: 381 us
  Pallas kernels  378 us (99%)
    pallas_call x1, Pallas kernels, step(): pl.pallas_call(functools.partial(kernel, side, tn, dt), out_shape=(jax.Sh...  378 us

profile of v3, /device:TPU:97, one launch (start us, length us, event | category | flops | bytes accessed | tf_op | source)
XLA Modules:
  0.0 380.9 jit_solution(9555232293195470512)
XLA Ops:
  0.0 377.8 %mlp.1 = (bf16[128,8192]{1,0:T(8,128)(2,1)}, bf16[2,4,512,8192]{3,2,1,0:T(8,128)(2,1)}, bf16[1536,8192]{1,0:T(8,128)(2,1)}, bf16[3,8,512,1024]{3,2,1,0:T(8,128)(2,1)}) custom-call(bf16[128,8192]{1,0:T(8,128)(2,1)} %x.1, bf16[8192,1536]{1,0:T(8,128)(2,1)} %wg.1, bf16[8192,1536]{1,0:T(8,128)(2,1)} %wu.1, bf16[1536,8192]{1,0:T(8,128)(2,1)} %wd.1), custom_call_target="tpu_custom_call" | custom-call | flops 309237645312 | bytes 452984832 | tf_op jit(solution)/shard_map/mlp/pallas_call | solution.py:662
  377.8 3.1 copy.6

commit v4 on v3

--- a/solution.py
+++ b/solution.py
@@ -105,6 +105,10 @@
                 hand(k, 2 * pair + q, hf).wait_recv()
         load(xb, slot, i * seg, xs.at[other, k, pl.ds(hf * half_rows + pair * seg, seg)], seg, slot)
 
+    def load_one(xb, slot, i, k, j, hf):
+        hand(k, j, hf).wait_recv()
+        load(xb, slot, i * seg + (j % 2) * hr, piece(k, j, hf, 1), hr, slot)
+
     def u_part(n, z, slot):
         cols, depth = pl.ds(pl.multiple_of(n * tn, tn), tn), pl.ds(z * (d // 2), d // 2)
         return [pltpu.make_async_copy(w.at[depth, cols], wbuf.at[slot, i, depth], wsem.at[slot, z]) for i, w in enumerate((wg, wu))]
@@ -169,6 +173,10 @@
     def w_piece(i):
         r = pl.ds(i * (hid // pieces), hid // pieces)
         return remote(wd.at[r], wp.at[r], wp_s, wp_r, sib)
+
+    def w_pieces(lo, hi):
+        for i in range(lo, hi):
+            w_piece(i).start()
 
     def hidden(lhs, ws):
         gate = jnp.dot(lhs[...], wbuf[ws, 0], preferred_element_type=F32)
@@ -344,22 +352,20 @@
         load_mid(xb, 1, 1)
 
         def hook(i):
-            pass
+            on(i, 1, (w_pieces, 0, 1))
 
         u_small(xb, 1, 2 * seg, 2, (half_rows + seg, half_rows + seg + hr), (row0(1, 1), row0(2, 1)), 1, hook, cuts[1], True, 1)
 
         def hook(i):
-            @when(i < cuts[1] + 2)
-            def _():
-                for q in range(2):
-                    w_piece(2 * (i - cuts[1]) + q).start()
-
+            on(i, cuts[1], (w_pieces, 1, 3))
+            on(i, nt - 3, (w_pieces, 3, 4))
             on(i, nt - 2, (forward, 0, 2), (push, 1, 0))
-            on(i, nt - 1, (push, 1, 1), (load_pair, xb, 0, 0, 0, 1, 0, 0), (load_pair, xb, 0, 1, 0, 1, 0, 1))
+            on(i, nt - 1, (push, 1, 1), (load_pair, xb, 0, 0, 0, 1, 0, 0), (load_pair, xb, 0, 1, 0, 1, 0, 1),
+               (load_one, xb, 0, 2, 1, 0, 0), (load_one, xb, 0, 3, 1, 0, 1))
 
         u_big(xb, (seg, half_rows + seg), (row0(1, 0), row0(1, 1)), 1, hook, cuts[1])
         for hf in range(2):
-            load_pair(xb, 0, 2 + hf, 1, 1, 0, hf)
+            load_one(xb, 0, 2 + hf, 1, 1, hf)
 
         def one_round(k, carry):
             fi = 2 // (k + 1)
@@ -372,34 +378,37 @@
 
                 @when(first)
                 def _():
-                    @when(it < pieces // 3)
-                    def _():
-                        w_piece(pieces // 3 + it).start()
-
-                    @when((it > nt) & (it <= nt + pieces // 3))
-                    def _():
-                        w_piece(2 * (pieces // 3) + it - nt - 1).start()
-
                     def keep(c):
                         return (c * seg, half_rows + c * seg)
 
                     def where(c):
                         return (row0(2 * c, 0), row0(2 * c, 1))
 
-                    on(it, 0, (h_sent, 0, hr))
-                    on(it, 0, (far, 1, 0))
-                    on(it, 1, (push, 1, 2), (far, 1, 1))
-                    on(it, 4, (push, 1, 3), (forward, 1, 0))
-                    on(it, 5, (load_pair, xb, 1, 0, 0, 1, 1, 0), (load_pair, xb, 1, 1, 0, 1, 1, 1),
-                       (load_pair, xb, 1, 2, 1, 1, 1, 0), (load_pair, xb, 1, 3, 1, 1, 1, 1))
-                    on(it, nt, (h_push, hk, 3, parts - 1, keep(0), where(0), seg), (h_sent, 1, seg), (forward, 1, 1))
-                    on(it, 7, (forward, 1, 2))
-                    on(it, 8, (forward, 1, 3))
-                    on(it, 9, (push, 2, 0))
-                    on(it, 11, (push, 2, 1))
-                    for part in range(parts - 1):
-                        for c in range(2):
+                    def h_parts(c):
+                        for part in range(parts - 1):
                             on(it, c * nt + cuts[part + 1], (h_push, hk, 3 + c, part, keep(c), where(c), seg))
+
+                    @when(it < nt)
+                    def _():
+                        on(it, 0, (h_sent, 0, hr), (far, 1, 0), (w_pieces, 4, 5))
+                        on(it, 1, (push, 1, 2), (far, 1, 1))
+                        on(it, 4, (push, 1, 3), (forward, 1, 0), (load_pair, xb, 1, 0, 0, 1, 1, 0), (load_pair, xb, 1, 1, 0, 1, 1, 1),
+                           (w_pieces, 5, 6))
+                        on(it, 5, (w_pieces, 6, 8), (load_pair, xb, 1, 2, 1, 1, 1, 0), (load_pair, xb, 1, 3, 1, 1, 1, 1))
+                        h_parts(0)
+
+                    @when(it >= nt)
+                    def _():
+                        @when(it < pieces - 2)
+                        def _():
+                            w_piece(it + 2).start()
+
+                        on(it, nt, (h_push, hk, 3, parts - 1, keep(0), where(0), seg), (h_sent, 1, seg), (forward, 1, 1))
+                        on(it, 7, (forward, 1, 2))
+                        on(it, 8, (forward, 1, 3))
+                        on(it, 9, (push, 2, 0))
+                        on(it, 11, (push, 2, 1))
+                        h_parts(1)
 
                 @when(k > 1)
                 def _():
@@ -506,12 +515,12 @@
 
                 @when(first)
                 def _():
-                    on(n, 0, (forward, 2, 0))
                     on(n, 1, (push, 2, 2))
-                    on(n, 2, (forward, 2, 1))
                     on(n, 4, (push, 2, 3))
-                    on(n, 5, (forward, 2, 2))
-                    on(n, 7, (forward, 2, 3))
+
+                    @when(lax.rem(n, 2) == 0)
+                    def _():
+                        forward(2, n // 2)
 
                 @when(k == 2)
                 def _():
@@ -519,13 +528,11 @@
                     on(n, 4, (push, 3, 3))
                     on(n, 7, (far, 0, 0), (far, 0, 1))
 
-                @when(k < 3)
-                def _():
-                    for v, other, pair in ((1, 0, 0), (3, 1, 0), (5, 0, 1), (6, 1, 1)):
-                        @when(n == v)
-                        def _():
-                            for hf in range(2):
-                                load_pair(xb, 1 - other, 2 * hf + pair, other, k + 1, pair, hf)
+                @when((k < 3) & ((n == 1) | (n == 3) | (n == 5) | (n == 6)))
+                def _():
+                    other, pair = lax.rem(n // 2, 2), n // (nd // 2)
+                    for hf in range(2):
+                        load_pair(xb, 1 - other, 2 * hf + pair, other, k + 1, pair, hf)
 
                 @when(k == 3)
                 def _():

time: 381 us -> 379 us (level)
  no operation moved by 1% of the time
where the time goes in v4:
time: 379 us; the launch traced here: 378 us
  Pallas kernels  375 us (99%)
    pallas_call x1, Pallas kernels, step(): pl.pallas_call(functools.partial(kernel, side, tn, dt), out_shape=(jax.Sh...  375 us

profile of v4, /device:TPU:97, one launch (start us, length us, event | category | flops | bytes accessed | tf_op | source)
XLA Modules:
  0.0 378.3 jit_solution(11992914526180437087)
XLA Ops:
  0.0 375.1 %mlp.1 = (bf16[128,8192]{1,0:T(8,128)(2,1)}, bf16[2,4,512,8192]{3,2,1,0:T(8,128)(2,1)}, bf16[1536,8192]{1,0:T(8,128)(2,1)}, bf16[3,8,512,1024]{3,2,1,0:T(8,128)(2,1)}) custom-call(bf16[128,8192]{1,0:T(8,128)(2,1)} %x.1, bf16[8192,1536]{1,0:T(8,128)(2,1)} %wg.1, bf16[8192,1536]{1,0:T(8,128)(2,1)} %wu.1, bf16[1536,8192]{1,0:T(8,128)(2,1)} %wd.1), custom_call_target="tpu_custom_call" | custom-call | flops 309237645312 | bytes 452984832 | tf_op jit(solution)/shard_map/mlp/pallas_call | solution.py:669
  375.2 3.1 copy.6

commit v5 on v4

--- a/solution.py
+++ b/solution.py
@@ -66,6 +66,14 @@
         move(piece(k, j, hf), k, j, hf, sib).wait_recv()
         hand(k, j, hf).start()
 
+    def landed(k, j):
+        for hf in range(2):
+            move(piece(k, j, hf), k, j, hf, sib).wait_recv()
+
+    def give(k, j):
+        for hf in range(2):
+            hand(k, j, hf).start()
+
     def push(k, j):
         for hf in range(2):
             arrive(k, j, hf)
@@ -111,21 +119,19 @@
 
     def u_part(n, z, slot):
         cols, depth = pl.ds(pl.multiple_of(n * tn, tn), tn), pl.ds(z * (d // 2), d // 2)
-        return [pltpu.make_async_copy(w.at[depth, cols], wbuf.at[slot, i, depth], wsem.at[slot, z]) for i, w in enumerate((wg, wu))]
+        return [pltpu.make_async_copy(w.at[depth, cols], wbuf.at[slot, depth, pl.ds(i * tn, tn)], wsem.at[slot, z])
+                for i, w in enumerate((wg, wu))]
 
     def u_copies(n, slot):
         return u_part(n, 0, slot) + u_part(n, 1, slot)
 
-    def d_rows(q):
-        return q // 2, (q % 2) * 2 * hid
-
     def d_copies(n, slot):
         r = []
-        for q in range(sub):
-            p, o = d_rows(q)
-            cols = pl.ds(pl.multiple_of(n * dt + q * tn, tn), tn)
+        for p in range(2):
+            cols = pl.ds(pl.multiple_of(n * dt + p * dt2, dt2), dt2)
             for i, w in enumerate((wd, wp)):
-                r.append(pltpu.make_async_copy(w.at[:, cols], wbuf.at[slot, p, pl.ds(o + i * hid, hid)], wsem.at[slot, 0]))
+                rows_p = pl.ds((2 * p + i) * hid, hid)
+                r.append(pltpu.make_async_copy(w.at[:, cols], wbuf.at[slot, rows_p], wsem.at[slot, 0]))
         return r
 
     def start(copies):
@@ -133,14 +139,14 @@
             cp.start()
 
     def held(slot, z, depth):
-        dst = wbuf.at[slot, :, depth]
+        dst = wbuf.at[slot, depth]
         pltpu.make_async_copy(dst, dst, wsem.at[slot, z]).wait()
 
     def u_held(z, slot):
         held(slot, z, pl.ds(z * (d // 2), d // 2))
 
     def d_held(slot):
-        held(slot, 0, pl.ds(0, sub * hid))
+        held(slot, 0, pl.ds(0, 4 * hid))
 
     def cut(part):
         return cuts[part] * tn, (cuts[part + 1] - cuts[part]) * tn
@@ -179,8 +185,8 @@
             w_piece(i).start()
 
     def hidden(lhs, ws):
-        gate = jnp.dot(lhs[...], wbuf[ws, 0], preferred_element_type=F32)
-        up = jnp.dot(lhs[...], wbuf[ws, 1], preferred_element_type=F32)
+        gate = jnp.dot(lhs[...], wbuf[ws, :, :tn], preferred_element_type=F32)
+        up = jnp.dot(lhs[...], wbuf[ws, :, tn:], preferred_element_type=F32)
         return (jax.nn.silu(gate) * up).astype(BF16)
 
     def u_cols(i):
@@ -226,7 +232,7 @@
                 u_held(z, ws)
                 depth = pl.ds(z * half, half)
                 lhs = xb[slot, pl.ds(row, 4 * hr), depth]
-                return [jnp.dot(lhs, wbuf[ws, q, depth], preferred_element_type=F32) for q in range(2)]
+                return [jnp.dot(lhs, wbuf[ws, depth, q * tn : (q + 1) * tn], preferred_element_type=F32) for q in range(2)]
 
             gate, up = products_of(0)
 
@@ -287,10 +293,9 @@
         in_copy(hop, n).start()
 
     def products(h, n, q):
-        p, o = d_rows(q)
         ws = lax.rem(n, 2)
         cols = slice(q * tn, (q + 1) * tn)
-        term = jnp.dot(h[...], wbuf[ws, p, pl.ds(o, 2 * hid)], preferred_element_type=F32)
+        term = jnp.dot(h[...], wbuf[ws, pl.ds((q // 2) * 2 * hid, 2 * hid), (q % 2) * tn : (q % 2 + 1) * tn], preferred_element_type=F32)
         return term + inb[lax.rem(n, 2), :, cols].astype(F32), cols
 
     def step_cols(e, base=0):
@@ -390,10 +395,11 @@
 
                     @when(it < nt)
                     def _():
-                        on(it, 0, (h_sent, 0, hr), (far, 1, 0), (w_pieces, 4, 5))
-                        on(it, 1, (push, 1, 2), (far, 1, 1))
+                        on(it, 0, (h_sent, 0, hr), (far, 1, 0))
+                        on(it, 1, (landed, 1, 2), (far, 1, 1))
+                        on(it, 2, (give, 1, 2))
                         on(it, 4, (push, 1, 3), (forward, 1, 0), (load_pair, xb, 1, 0, 0, 1, 1, 0), (load_pair, xb, 1, 1, 0, 1, 1, 1),
-                           (w_pieces, 5, 6))
+                           (w_pieces, 4, 6))
                         on(it, 5, (w_pieces, 6, 8), (load_pair, xb, 1, 2, 1, 1, 1, 0), (load_pair, xb, 1, 3, 1, 1, 1, 1))
                         h_parts(0)
 
@@ -617,7 +623,7 @@
                 add_near(e - 6)
 
             for q in range(2):
-                term = jnp.dot(h0[...], wbuf[ws, c2, pl.ds(q * 2 * hid, 2 * hid)], preferred_element_type=F32)
+                term = jnp.dot(h0[...], wbuf[ws, pl.ds(pl.multiple_of(c2 * 2 * hid, 2 * hid), 2 * hid), q * tn : (q + 1) * tn], preferred_element_type=F32)
                 cols = slice(q * tn, (q + 1) * tn)
                 total = term + inb[lax.rem(n, 2), :, pl.ds(pl.multiple_of(c2 * dt2 + q * tn, tn), tn)].astype(F32)
                 for hf in range(2):
@@ -677,7 +683,7 @@
             in_specs=[hbm] * 4,
             out_specs=[hbm] * 4,
             scratch_shapes=[
-                pltpu.VMEM((2, 2, d, tn), BF16),
+                pltpu.VMEM((2, d, 2 * tn), BF16),
                 pltpu.VMEM((m, 2 * hid), BF16),
                 pltpu.VMEM((2 * m, 2 * hid), BF16),
                 pltpu.VMEM((nd, m, dt), BF16),

time: 379 us -> 378 us (level)
  no operation moved by 1% of the time
where the time goes in v5:
time: 378 us
  Pallas kernels  375 us (99%)
    pallas_call x1, Pallas kernels, step(): pl.pallas_call(functools.partial(kernel, side, tn, dt), out_shape=(jax.Sh...  375 us

profile of v5, /device:TPU:97, one launch (start us, length us, event | category | flops | bytes accessed | tf_op | source)
XLA Modules:
  0.0 377.7 jit_solution(1122927329827026743)
XLA Ops:
  0.0 374.6 %mlp.1 = (bf16[128,8192]{1,0:T(8,128)(2,1)}, bf16[2,4,512,8192]{3,2,1,0:T(8,128)(2,1)}, bf16[1536,8192]{1,0:T(8,128)(2,1)}, bf16[3,8,512,1024]{3,2,1,0:T(8,128)(2,1)}) custom-call(bf16[128,8192]{1,0:T(8,128)(2,1)} %x.1, bf16[8192,1536]{1,0:T(8,128)(2,1)} %wg.1, bf16[8192,1536]{1,0:T(8,128)(2,1)} %wu.1, bf16[1536,8192]{1,0:T(8,128)(2,1)} %wd.1), custom_call_target="tpu_custom_call" | custom-call | flops 309237645312 | bytes 452984832 | tf_op jit(solution)/shard_map/mlp/pallas_call | solution.py:675
  374.6 3.1 copy.6
